TPU v7x, 32 devices: a whole 2x2x4 slice. The times are simulated.
32 devices in a mesh: clip: 2 (over y), outer: 4 (over z), inner: 2 (over x), head: 2 (over core).
Axes of the slice: x: 2, y: 2, z: 4, core: 2. Of those that a mesh axis runs over, the one named last changes fastest.
Arguments:
- tokens: bfloat16 [2, 4096, 3072], P('clip', ('outer', 'inner', 'head')), parts along dimension 0, may hold values from -6 to 6
- shift_mod: float32 [2, 3072], P('clip'), parts along dimension 0, may hold values from -3 to 3
- scale_mod: float32 [2, 3072], P('clip'), parts along dimension 0, may hold values from -1.5 to 1.5
- gate_mod: float32 [2, 3072], P('clip'), parts along dimension 0, may hold values from 0.5 to 2
- query_weight: bfloat16 [3072, 3072], P('outer', ('inner', 'head')), may hold values from -0.109375 to 0.109375
- key_weight: bfloat16 [3072, 3072], P('outer', ('inner', 'head')), may hold values from -0.109375 to 0.109375
- value_weight: bfloat16 [3072, 3072], P('outer', ('inner', 'head')), may hold values from -0.109375 to 0.109375
- out_weight: bfloat16 [3072, 3072], P(('inner', 'head'), 'outer'), may hold values from -0.109375 to 0.109375
- query_gain: float32 [128], replicated, may hold values from 1 to 18, as said below
- key_gain: float32 [128], replicated, may hold values from 1 to 18, as said below
Outputs:
- attended: bfloat16 [2, 4096, 3072], P('clip', ('outer', 'inner', 'head')), parts along dimension 0
There are 2 independent parts, one for each index of `clip`. A program takes and returns all parts, laid end to end along the dimension named above; an argument that names none is the same for every part. Nothing has to cross between parts.
Inputs may be any that keep to these rules, and one draw needn't show every extreme that they name: `query_gain`: 128 positive scales. `key_gain`: 128 positive scales.
All inputs are finite; a program needn't handle non-finite values.
Results may differ from a plain program's by a relative error of at most 0.015.
The roundings to bfloat16 on the way count: a program that leaves them out, or rounds other values in their place, can miss the bound.
Values may be sent and summed in bfloat16 or wider, within the bound.
A program may use at most 192 MiB of HBM per device.

v0:
```python
import math
import jax
import jax.numpy as jnp
from jax import lax
from jax.sharding import PartitionSpec as P

EPSILON = 1e-06


def modulate(tokens, shift_mod, scale_mod):
    values = tokens.astype(jnp.float32)
    center = jnp.mean(values, axis=-1, keepdims=True)
    spread = jnp.mean(jnp.square(values - center), axis=-1, keepdims=True)
    normed = (values - center) / jnp.sqrt(spread + EPSILON)
    return (normed * (1.0 + scale_mod[:, None, :]) + shift_mod[:, None, :]).astype(jnp.bfloat16)


def head_norm(projected, gain_vec, head_dim):
    shaped = projected.reshape(projected.shape[:-1] + (projected.shape[-1] // head_dim, head_dim))
    mean_square = jnp.mean(jnp.square(shaped), axis=-1, keepdims=True)
    return (shaped / jnp.sqrt(mean_square + EPSILON) * gain_vec).astype(jnp.bfloat16)


def per_device(
    tokens,
    shift_mod,
    scale_mod,
    gate_mod,
    query_weight,
    key_weight,
    value_weight,
    out_weight,
    query_gain,
    key_gain,
):
    head_dim = query_gain.shape[0]
    modulated = modulate(tokens, shift_mod, scale_mod)
    gathered = lax.all_gather(modulated, ("inner", "head"), axis=1, tiled=True)
    clip_count, row_count, model_width = gathered.shape
    flattened = gathered.reshape(clip_count * row_count, model_width)
    local_cols = query_weight.shape[1]
    head_count = local_cols // head_dim
    full_query, full_key, full_value = (
        lax.all_gather(query_weight, "outer", axis=0, tiled=True),
        lax.all_gather(key_weight, "outer", axis=0, tiled=True),
        lax.all_gather(value_weight, "outer", axis=0, tiled=True),
    )
    query_proj = jnp.dot(flattened, full_query, preferred_element_type=jnp.float32)
    key_proj = jnp.dot(flattened, full_key, preferred_element_type=jnp.float32)
    value_proj = jnp.dot(flattened, full_value, preferred_element_type=jnp.float32)
    query_heads = head_norm(
        query_proj.reshape(clip_count, row_count, local_cols), query_gain, head_dim
    )
    key_send = head_norm(key_proj.reshape(clip_count, row_count, local_cols), key_gain, head_dim)
    key_send = key_send.reshape(clip_count, row_count, local_cols)
    value_send = value_proj.astype(jnp.bfloat16).reshape(clip_count, row_count, local_cols)
    root_size = math.sqrt(head_dim)
    full_out = lax.all_gather(out_weight, "outer", axis=1, tiled=True)
    running_max = jnp.full((clip_count, head_count, row_count), -1e30, jnp.float32)
    key_piece = lax.all_gather(key_send, "outer", axis=1, tiled=True)
    value_piece = lax.all_gather(value_send, "outer", axis=1, tiled=True)
    key_count = key_piece.shape[1]
    key_piece = key_piece.reshape(clip_count, key_count, head_count, head_dim)
    value_piece = value_piece.reshape(clip_count, key_count, head_count, head_dim)
    scores = (
        jnp.einsum("cqhd,ckhd->chqk", query_heads, key_piece, preferred_element_type=jnp.float32)
        / root_size
    )
    new_max = jnp.maximum(running_max, jnp.max(scores, axis=-1))
    weights = jnp.exp(scores - new_max[..., None])
    new_sum = jnp.sum(weights, axis=-1)
    new_acc = jnp.einsum(
        "chqk,ckhd->chqd",
        weights.astype(jnp.bfloat16),
        value_piece,
        preferred_element_type=jnp.float32,
    )
    head_out = new_acc / new_sum[..., None]
    mixed = (
        jnp.transpose(head_out, (0, 2, 1, 3))
        .reshape(clip_count * row_count, local_cols)
        .astype(jnp.bfloat16)
    )
    partial_value = jnp.dot(mixed, full_out, preferred_element_type=jnp.float32).reshape(
        clip_count, row_count, -1
    )
    summed = lax.psum_scatter(
        partial_value.astype(jnp.bfloat16), ("inner", "head"), scatter_dimension=1, tiled=True
    ).astype(jnp.float32)
    return (summed * gate_mod[:, None, :]).astype(jnp.bfloat16)


def solution(mesh):
    in_specs = (
        P("clip", ("outer", "inner", "head"), None),
        P("clip", None),
        P("clip", None),
        P("clip", None),
        P("outer", ("inner", "head")),
        P("outer", ("inner", "head")),
        P("outer", ("inner", "head")),
        P(("inner", "head"), "outer"),
        P(),
        P(),
    )
    out_specs = P("clip", ("outer", "inner", "head"), None)
    return jax.shard_map(
        per_device, mesh=mesh, in_specs=in_specs, out_specs=out_specs, check_vma=False
    )
```

profile of v0, /device:TPU:0, one launch (start us, length us, event | category | flops | bytes accessed | tf_op | source)
XLA Modules:
  0.0 723.6 jit_solution(17213850684140932397)
XLA Ops:
  6.5 0.0 copy-start
  6.5 0.0 copy-start.2
  6.5 0.0 copy-start.6
  6.5 0.0 copy-start.4
  6.5 0.0 all-gather.14.cloned.1.call-start
  6.6 0.7 all-gather.14.cloned.1.call-update
  7.3 0.0 all-gather.10.cloned.1.call-start
  7.3 1.7 convert_reduce_fusion
  9.0 0.0 copy-done.2
  9.0 0.6 fusion.12
  9.6 0.0 copy-done.6
  9.6 0.0 copy-done.4
  9.6 1.9 fusion.15
  11.6 0.0 all-gather.10.cloned.1.call-update
  11.6 0.0 all-gather.16.cloned.1.call-start
  11.7 0.7 all-gather.16.cloned.1.call-update
  12.3 0.0 all-gather.12.cloned.1.call-start
  12.4 0.5 all-gather.12.cloned.1.call-update
  12.9 0.0 all-gather.20.cloned.1.call-start
  13.0 0.0 copy-done
  13.0 88.1 %all-gather.14.cloned.1.call-done = bf16[3072,768]{1,0:T(8,128)(2,1)} async-done(((bf16[768,768]{1,0:T(8,128)(2,1)}), bf16[3072,768]{1,0:T(8,128)(2,1)}) %all-gather.14.cloned.1.call-update) | async-done | bytes 4718608 | tf_op jit(solution)/shard_map/all_gather | solution.py:45
  101.1 46.4 %all-gather.10.cloned.1.call-done = bf16[1,1024,3072]{2,1,0:T(8,128)(2,1)} async-done(((bf16[1,256,3072]{2,1,0:T(8,128)(2,1)}), bf16[1,1024,3072]{2,1,0:T(8,128)(2,1)}) %all-gather.10.cloned.1.call-update) | async-done | bytes 6291472 | tf_op jit(solution)/shard_map/all_gather | solution.py:38
  147.4 9.8 %fusion.27 = (f32[1024,768]{0,1:T(8,128)S(1)}, f32[1024,768]{0,1:T(8,128)}) fusion(bf16[3072,768]{1,0:T(8,128)(2,1)} %all-gather.14.cloned.1.call-done, bf16[1,1024,3072]{2,1,0:T(8,128)(2,1)} %all-gather.10.cloned.1.call-done), kind=kOutput, calls=%fused_computation.38 | convolution fusion | flops 4832624640 | bytes 17301504 | tf_op jit(solution)/shard_map/dot_general | solution.py:49
  157.2 0.3 reduce_sum.48
  157.5 3.6 fusion.17
  161.1 0.0 all-gather.20.cloned.1.call-update
  161.2 0.0 all-gather.22.cloned.1.call-start
  161.2 77.2 %all-gather.16.cloned.1.call-done = bf16[3072,768]{1,0:T(8,128)(2,1)} async-done(((bf16[768,768]{1,0:T(8,128)(2,1)}), bf16[3072,768]{1,0:T(8,128)(2,1)}) %all-gather.16.cloned.1.call-update) | async-done | bytes 4718608 | tf_op jit(solution)/shard_map/all_gather | solution.py:46
  238.4 9.4 %fusion.20 = bf16[1024,768]{1,0:T(8,128)(2,1)} fusion(bf16[3072,768]{1,0:T(8,128)(2,1)} %all-gather.16.cloned.1.call-done, bf16[1,1024,3072]{2,1,0:T(8,128)(2,1)} %all-gather.10.cloned.1.call-done), kind=kOutput, calls=%fused_computation.26 | convolution fusion | flops 4832624640 | bytes 12582912 | tf_op jit(solution)/shard_map/dot_general | solution.py:50
  247.8 0.0 all-gather.22.cloned.1.call-update
  247.8 0.0 all-gather.18.cloned.1.call-start
  247.9 0.7 all-gather.18.cloned.1.call-update
  248.6 0.2 reduce-scatter.2.cloned.1.call-start
  248.8 78.9 %all-gather.12.cloned.1.call-done = bf16[3072,768]{1,0:T(8,128)(2,1)} async-done(((bf16[768,768]{1,0:T(8,128)(2,1)}), bf16[3072,768]{1,0:T(8,128)(2,1)}) %all-gather.12.cloned.1.call-update) | async-done | bytes 4718608 | tf_op jit(solution)/shard_map/all_gather | solution.py:44
  327.7 10.3 %fusion.28 = (f32[1024,768]{0,1:T(8,128)}, f32[1024,768]{0,1:T(8,128)}) fusion(bf16[3072,768]{1,0:T(8,128)(2,1)} %all-gather.12.cloned.1.call-done, bf16[1,1024,3072]{2,1,0:T(8,128)(2,1)} %all-gather.10.cloned.1.call-done), kind=kOutput, calls=%fused_computation.39 | convolution fusion | flops 4832624640 | bytes 17301504 | tf_op jit(solution)/shard_map/dot_general | solution.py:48
  338.0 2.6 copy.14
  340.6 0.0 copy-start.3
  340.6 2.2 reduce_sum.47
  342.9 100.0 %all-gather.20.cloned.1.call-done = bf16[4096,768]{0,1:T(8,128)(2,1)} async-done(((bf16[1024,768]{0,1:T(8,128)(2,1)}), bf16[4096,768]{0,1:T(8,128)(2,1)}) %all-gather.20.cloned.1.call-update) | async-done | bytes 6291472 | tf_op jit(solution)/shard_map/all_gather | solution.py:60
  442.9 0.0 copy-done.3
  442.9 39.0 %multiply_reduce_fusion = (f32[6,1024]{1,0:T(8,128)S(1)}, f32[6,1024,4096]{2,1,0:T(8,128)}) fusion(bf16[4096,6,128]{0,2,1:T(8,128)(2,1)} %bitcast.44, f32[1024,6,128]{2,0,1:T(8,128)S(1)} %copy.14, f32[128]{0:T(128)S(1)} %copy-done.3, f32[1024,6]{0,1:T(8,128)S(1)} %add_sqrt_fusion.1), kind=kOutput, calls=%fused_computation.1 | convolution fusion | flops 6495135744 | bytes 110150144 | tf_op jit(solution)/shard_map/cqhd,ckhd->chqk/dot_general | solution.py:66
  481.9 76.0 %all-gather.22.cloned.1.call-done = bf16[4096,768]{1,0:T(8,128)(2,1)} async-done(((bf16[1024,768]{1,0:T(8,128)(2,1)}), bf16[4096,768]{1,0:T(8,128)(2,1)}) %all-gather.22.cloned.1.call-update) | async-done | bytes 6291472 | tf_op jit(solution)/shard_map/all_gather | solution.py:61
  557.9 8.8 %copy.16 = bf16[4096,768]{0,1:T(8,128)(2,1)} copy(bf16[4096,768]{1,0:T(8,128)(2,1)} %all-gather.22.cloned.1.call-done) | data formatting | bytes 12582912 | tf_op jit(solution)/shard_map/all_gather | solution.py:61
  566.6 31.5 %fusion = f32[6,1024]{1,0:T(8,128)S(1)} fusion(f32[6,1024,4096]{2,1,0:T(8,128)} %get-tuple-element.10, f32[6,1024]{1,0:T(8,128)S(1)} %broadcast_maximum_fusion), kind=kLoop, calls=%fused_computation.2 | loop fusion | flops 75491328 | bytes 100712448 | tf_op jit(solution)/shard_map/reduce_sum | solution.py:71
  598.1 35.6 %divide_convert_fusion = bf16[6,1024,128]{1,2,0:T(8,128)(2,1)S(1)} fusion(bf16[4096,6,128]{0,2,1:T(8,128)(2,1)} %bitcast.43, f32[6,1024,4096]{2,1,0:T(8,128)} %get-tuple-element.10, f32[6,1024]{1,0:T(8,128)S(1)} %broadcast_maximum_fusion, f32[6,1024]{1,0:T(8,128)S(1)} %fusion), kind=kOutput, calls=%fused_computation.24 | convolution fusion | flops 6519521280 | bytes 108576768 | tf_op jit(solution)/shard_map/chqk,ckhd->chqd/dot_general | solution.py:72
  633.7 13.3 %all-gather.18.cloned.1.call-done = bf16[768,3072]{1,0:T(8,128)(2,1)} async-done(((bf16[768,768]{1,0:T(8,128)(2,1)}), bf16[768,3072]{1,0:T(8,128)(2,1)}) %all-gather.18.cloned.1.call-update) | async-done | bytes 4718608 | tf_op jit(solution)/shard_map/all_gather | solution.py:58
  647.0 9.4 %convert_bitcast_fusion = bf16[1,1024,3072]{2,1,0:T(8,128)(2,1)} fusion(bf16[1024,768]{0,1:T(8,128)(2,1)S(1)} %bitcast.51, bf16[768,3072]{1,0:T(8,128)(2,1)} %all-gather.18.cloned.1.call-done), kind=kOutput, calls=%fused_computation.11 | convolution fusion | flops 4834983936 | bytes 12582912 | tf_op jit(solution)/shard_map/dot_general | solution.py:84
  656.4 0.0 copy-start.5
  656.4 0.0 reduce-scatter.2.cloned.1.call-update
  656.4 0.0 copy-start.1
  656.5 57.4 %reduce-scatter.2.cloned.1.call-done = bf16[1,256,3072]{2,1,0:T(8,128)(2,1)} async-done(((bf16[1,1024,3072]{2,1,0:T(8,128)(2,1)}), bf16[1,256,3072]{2,1,0:T(8,128)(2,1)}) %reduce-scatter.2.cloned.1.call-update) | async-done | bytes 1572880 | tf_op jit(solution)/shard_map/reduce_scatter | solution.py:87
  713.8 0.0 copy-done.5
  713.8 2.9 multiply_convert_fusion
  716.7 0.0 copy-done.1
  (7 shorter events, 0.1 us)
Async XLA Ops:
  6.5 6.4 copy-start
  6.5 2.5 copy-start.2
  6.5 3.1 copy-start.6
  6.5 3.1 copy-start.4
  6.5 94.5 %all-gather.14.cloned.1.call-start = ((), (), s32[]{:S(2)}) async-start(), calls=%async_computation.3 | async-start | bytes 5898240 | tf_op jit(solution)/shard_map/all_gather | solution.py:45
  7.3 140.1 %all-gather.10.cloned.1.call-start = ((), (), s32[]{:S(2)}) async-start(), calls=%async_computation.1 | async-start | bytes 7864320 | tf_op jit(solution)/shard_map/all_gather | solution.py:38
  11.6 226.8 %all-gather.16.cloned.1.call-start = ((), (), s32[]{:S(2)}) async-start(), calls=%async_computation.4 | async-start | bytes 5898240 | tf_op jit(solution)/shard_map/all_gather | solution.py:46
  12.3 315.3 %all-gather.12.cloned.1.call-start = ((), (), s32[]{:S(2)}) async-start(), calls=%async_computation.2 | async-start | bytes 5898240 | tf_op jit(solution)/shard_map/all_gather | solution.py:44
  12.9 430.0 %all-gather.20.cloned.1.call-start = ((), (), s32[]{:S(2)}) async-start(), calls=%async_computation.7 | async-start | bytes 7864320 | tf_op jit(solution)/shard_map/all_gather | solution.py:60
  161.2 396.7 %all-gather.22.cloned.1.call-start = ((), (), s32[]{:S(2)}) async-start(), calls=%async_computation.8 | async-start | bytes 7864320 | tf_op jit(solution)/shard_map/all_gather | solution.py:61
  247.8 399.2 %all-gather.18.cloned.1.call-start = ((), (), s32[]{:S(2)}) async-start(), calls=%async_computation.5 | async-start | bytes 5898240 | tf_op jit(solution)/shard_map/all_gather | solution.py:58
  248.6 465.3 %reduce-scatter.2.cloned.1.call-start = ((), (), s32[]{:S(2)}) async-start(), calls=%async_computation.6 | async-start | bytes 7864320 | tf_op jit(solution)/shard_map/reduce_scatter | solution.py:87
  340.6 102.2 %copy-start.3 = (f32[128]{0:T(128)S(1)}, f32[128]{0:T(128)}, u32[]{:S(2)}) copy-start(f32[128]{0:T(128)} %param.18) | copy-start | bytes 1540
  656.4 57.4 %copy-start.5 = (f32[1,3072]{1,0:T(1,128)S(1)}, f32[1,3072]{1,0:T(1,128)}, u32[]{:S(2)}) copy-start(f32[1,3072]{1,0:T(1,128)} %param.13) | copy-start | bytes 36868
  656.4 60.3 %copy-start.1 = (f32[128]{0:T(128)S(1)}, f32[128]{0:T(128)}, u32[]{:S(2)}) copy-start(f32[128]{0:T(128)} %param.19) | copy-start | bytes 1540
Sparse Core Ops, SparseCore 0:
  8.9 92.0 all-gather.13
  102.6 44.7 all-gather.9
  149.0 89.3 all-gather.15
  239.8 87.7 all-gather.11
  329.1 113.7 all-gather.19
  444.3 113.5 all-gather.21
  559.4 87.5 all-gather.17
  656.6 57.2 reduce-scatter.1
where the time goes:
time: 724 us
  waiting for transfers between devices  540 us (75%)
  matrix products  113 us (16%)
  other arithmetic  44.7 us (6%)
  between operations  13.6 us (2%)
  local copies, waits for them, and re-layouts  11.4 us (2%)
    all_gather x1, waiting for transfers between devices, per_device(): key_piece = lax.all_gather(key_send, 'outer', axis=1, tiled=True)  100 us
    all_gather x1, waiting for transfers between devices, per_device(): lax.all_gather(key_weight, 'outer', axis=0, tiled=True)  88.1 us
    all_gather x1, waiting for transfers between devices, per_device(): lax.all_gather(query_weight, 'outer', axis=0, tiled=True)  78.9 us
    all_gather x1, waiting for transfers between devices, per_device(): lax.all_gather(value_weight, 'outer', axis=0, tiled=True)  77.2 us
    all_gather x1, waiting for transfers between devices, per_device(): value_piece = lax.all_gather(value_send, 'outer', axis=1, tiled=True)  76 us
    reduce_scatter x1, waiting for transfers between devices, per_device(): lax.psum_scatter(partial_value.astype(jnp.bfloat16), ('inner', 'head'), s...  57.4 us
    all_gather x1, waiting for transfers between devices, per_device(): gathered = lax.all_gather(modulated, ('inner', 'head'), axis=1, tiled=True)  46.4 us
    dot_general x1, matrix products, per_device(): jnp.einsum('cqhd,ckhd->chqk', query_heads, key_piece, preferred_element_t...  39 us
  transfers between devices with their start and end apart: 8, of which 8 were waited for; matrix products, arithmetic and copies ran while one was open for 22% of the time, Pallas kernels for 0%

commit v1 on v0

--- a/solution.py
+++ b/solution.py
@@ -5,6 +5,16 @@
 from jax.sharding import PartitionSpec as P
 
 EPSILON = 1e-06
+
+
+def around_the_ring(x, axis, along):
+    size = lax.axis_size(axis)
+    held, blocks = (x, [x])
+    for _ in range(size - 1):
+        held = lax.ppermute(held, axis, [(i, (i + 1) % size) for i in range(size)])
+        blocks.insert(0, held)
+    row_of_blocks = jnp.concatenate(blocks, axis=along)
+    return jnp.roll(row_of_blocks, (lax.axis_index(axis) + 1) * x.shape[along], axis=along)
 
 
 def modulate(tokens, shift_mod, scale_mod):
@@ -57,7 +67,7 @@
     root_size = math.sqrt(head_dim)
     full_out = lax.all_gather(out_weight, "outer", axis=1, tiled=True)
     running_max = jnp.full((clip_count, head_count, row_count), -1e30, jnp.float32)
-    key_piece = lax.all_gather(key_send, "outer", axis=1, tiled=True)
+    key_piece = around_the_ring(key_send, "outer", 1)
     value_piece = lax.all_gather(value_send, "outer", axis=1, tiled=True)
     key_count = key_piece.shape[1]
     key_piece = key_piece.reshape(clip_count, key_count, head_count, head_dim)

time: 724 us -> 730 us (level)
  waiting for transfers between devices: 540 us -> 493 us
  starting transfers between devices: 0.49 us -> 42.2 us
  local copies, waits for them, and re-layouts: 11.4 us -> 22.1 us
    ppermute x0 -> x3, waiting for transfers between devices: none -> 188 us  [around_the_ring(): held = lax.ppermute(held, axis, [(i, (i + 1) % size) for i in range(size)])]
    all_gather x1 -> x0, waiting for transfers between devices: 100 us -> none  [per_device(): key_piece = lax.all_gather(key_send, 'outer', axis=1, tiled=True)]
    all_gather x1, waiting for transfers between devices: 78.9 us -> 0.01 us  [per_device(): lax.all_gather(query_weight, 'outer', axis=0, tiled=True)]
    all_gather x1, waiting for transfers between devices: 76 us -> 0.02 us  [per_device(): value_piece = lax.all_gather(value_send, 'outer', axis=1, tiled=True)]
    ppermute x0 -> x3, starting transfers between devices: none -> 42 us  [around_the_ring(): held = lax.ppermute(held, axis, [(i, (i + 1) % size) for i in range(size)])]
    reduce_scatter x1, waiting for transfers between devices: 57.4 us -> 89.4 us  [per_device(): lax.psum_scatter(partial_value.astype(jnp.bfloat16), ('inner', 'head'), s...]
    all_gather x1, waiting for transfers between devices: 13.3 us -> 0.02 us  [per_device(): full_out = lax.all_gather(out_weight, 'outer', axis=1, tiled=True)]
    all_gather x1, waiting for transfers between devices: 77.2 us -> 85.3 us  [per_device(): lax.all_gather(value_weight, 'outer', axis=0, tiled=True)]
  transfers between devices with their start and end apart: 8 -> 10, of which waited for: 8 -> 7; matrix products, arithmetic and copies ran while one was open for 22% -> 23% of each run, Pallas kernels for 0% -> 0%
where the time goes in v1:
time: 730 us
  waiting for transfers between devices  493 us (68%)
  matrix products  113 us (15%)
  other arithmetic  46 us (6%)
  starting transfers between devices  42.2 us (6%)
  local copies, waits for them, and re-layouts  22.1 us (3%)
  between operations  13.7 us (2%)
    ppermute x3, waiting for transfers between devices, around_the_ring(): held = lax.ppermute(held, axis, [(i, (i + 1) % size) for i in range(size)])  188 us
    reduce_scatter x1, waiting for transfers between devices, per_device(): lax.psum_scatter(partial_value.astype(jnp.bfloat16), ('inner', 'head'), s...  89.4 us
    all_gather x1, waiting for transfers between devices, per_device(): lax.all_gather(value_weight, 'outer', axis=0, tiled=True)  85.3 us
    all_gather x1, waiting for transfers between devices, per_device(): lax.all_gather(key_weight, 'outer', axis=0, tiled=True)  81.5 us
    all_gather x1, waiting for transfers between devices, per_device(): gathered = lax.all_gather(modulated, ('inner', 'head'), axis=1, tiled=True)  46.4 us
    ppermute x3, starting transfers between devices, around_the_ring(): held = lax.ppermute(held, axis, [(i, (i + 1) % size) for i in range(size)])  42 us
    dot_general x1, matrix products, per_device(): jnp.einsum('cqhd,ckhd->chqk', query_heads, key_piece, preferred_element_t...  38.7 us
    dot_general x1, matrix products, per_device(): jnp.einsum('chqk,ckhd->chqd', weights.astype(jnp.bfloat16), value_piece,...  35.3 us
  transfers between devices with their start and end apart: 10, of which 7 were waited for; matrix products, arithmetic and copies ran while one was open for 23% of the time, Pallas kernels for 0%

profile of v1, /device:TPU:0, one launch (start us, length us, event | category | flops | bytes accessed | tf_op | source)
XLA Modules:
  0.0 729.7 jit_solution(14159863932915718971)
XLA Ops:
  6.5 0.0 copy-start
  6.5 0.0 copy-start.2
  6.5 0.0 all-gather.14.cloned.1.call-start
  6.5 0.7 all-gather.14.cloned.1.call-update
  7.3 0.0 all-gather.8.cloned.1.call-start
  7.3 1.7 convert_reduce_fusion
  9.0 2.0 fusion.12
  11.0 0.7 broadcast_add_fusion
  11.7 0.0 copy-done.2
  11.7 2.6 fusion.15
  14.4 0.0 all-gather.8.cloned.1.call-update
  14.4 0.0 all-gather.12.cloned.1.call-start
  14.4 0.7 all-gather.12.cloned.1.call-update
  15.1 0.0 all-gather.10.cloned.1.call-start
  15.2 0.5 all-gather.10.cloned.1.call-update
  15.7 0.0 all-gather.18.cloned.1.call-start
  15.8 85.3 %all-gather.14.cloned.1.call-done = bf16[3072,768]{1,0:T(8,128)(2,1)} async-done(((bf16[768,768]{1,0:T(8,128)(2,1)}), bf16[3072,768]{1,0:T(8,128)(2,1)}) %all-gather.14.cloned.1.call-update) | async-done | bytes 4718608 | tf_op jit(solution)/shard_map/all_gather | solution.py:56
  101.0 46.4 %all-gather.8.cloned.1.call-done = bf16[1,1024,3072]{2,1,0:T(8,128)(2,1)} async-done(((bf16[1,256,3072]{2,1,0:T(8,128)(2,1)}), bf16[1,1024,3072]{2,1,0:T(8,128)(2,1)}) %all-gather.8.cloned.1.call-update) | async-done | bytes 6291472 | tf_op jit(solution)/shard_map/all_gather | solution.py:48
  147.4 9.4 %fusion.20 = bf16[1024,768]{1,0:T(8,128)(2,1)} fusion(bf16[3072,768]{1,0:T(8,128)(2,1)} %all-gather.14.cloned.1.call-done, bf16[1,1024,3072]{2,1,0:T(8,128)(2,1)} %all-gather.8.cloned.1.call-done), kind=kOutput, calls=%fused_computation.26 | convolution fusion | flops 4832624640 | bytes 12582912 | tf_op jit(solution)/shard_map/dot_general | solution.py:60
  156.8 0.0 all-gather.18.cloned.1.call-update
  156.8 0.0 all-gather.16.cloned.1.call-start
  156.9 0.0 copy-done
  156.9 81.5 %all-gather.12.cloned.1.call-done = bf16[3072,768]{1,0:T(8,128)(2,1)} async-done(((bf16[768,768]{1,0:T(8,128)(2,1)}), bf16[3072,768]{1,0:T(8,128)(2,1)}) %all-gather.12.cloned.1.call-update) | async-done | bytes 4718608 | tf_op jit(solution)/shard_map/all_gather | solution.py:55
  238.4 9.8 %fusion.27 = (f32[1024,768]{0,1:T(8,128)S(1)}, f32[1024,768]{0,1:T(8,128)}) fusion(bf16[3072,768]{1,0:T(8,128)(2,1)} %all-gather.12.cloned.1.call-done, bf16[1,1024,3072]{2,1,0:T(8,128)(2,1)} %all-gather.8.cloned.1.call-done), kind=kOutput, calls=%fused_computation.47 | convolution fusion | flops 4832624640 | bytes 17301504 | tf_op jit(solution)/shard_map/dot_general | solution.py:59
  248.3 0.3 reduce_sum.48
  248.6 2.3 fusion.17
  250.9 0.1 collective-permute-start
  250.9 72.4 %collective-permute-done = bf16[1,1024,768]{1,2,0:T(8,128)(2,1)S(1)} collective-permute-done((bf16[1,1024,768]{1,2,0:T(8,128)(2,1)S(1)}, bf16[1,1024,768]{1,2,0:T(8,128)(2,1)S(1)}, u32[]{:S(2)}, u32[]{:S(2)}) %collective-permute-start) | collective-permute-done | bytes 1572896 | tf_op jit(solution)/shard_map/ppermute | solution.py:14
  323.4 28.8 %collective-permute-start.1 = (bf16[1,1024,768]{1,2,0:T(8,128)(2,1)S(1)}, bf16[1,1024,768]{1,2,0:T(8,128)(2,1)}, u32[]{:S(2)}, u32[]{:S(2)}) collective-permute-start(bf16[1,1024,768]{1,2,0:T(8,128)(2,1)S(1)} %collective-permute-done), channel_id=1, source_target_pairs={{0,4},{4,8},{8,12},{12,0},{1,5},{5,9},{9,13},{13,1},{2,6},{6,10},{... | collective-permute-start | bytes 4718600 | tf_op jit(solution)/shard_map/ppermute | solution.py:14
  352.2 0.0 all-gather.16.cloned.1.call-update
  352.2 0.0 reduce-scatter.2.cloned.1.call-start
  352.3 59.6 %collective-permute-done.1 = bf16[1,1024,768]{1,2,0:T(8,128)(2,1)} collective-permute-done((bf16[1,1024,768]{1,2,0:T(8,128)(2,1)S(1)}, bf16[1,1024,768]{1,2,0:T(8,128)(2,1)}, u32[]{:S(2)}, u32[]{:S(2)}) %collective-permute-start.1) | collective-permute-done | bytes 1572896 | tf_op jit(solution)/shard_map/ppermute | solution.py:14
  411.9 13.1 %collective-permute-start.2 = (bf16[1,1024,768]{1,2,0:T(8,128)(2,1)}, bf16[1,1024,768]{1,2,0:T(8,128)(2,1)}, u32[]{:S(2)}, u32[]{:S(2)}) collective-permute-start(bf16[1,1024,768]{1,2,0:T(8,128)(2,1)} %collective-permute-done.1), channel_id=1, source_target_pairs={{0,4},{4,8},{8,12},{12,0},{1,5},{5,9},{9,13},{13,1},{2,6},{6,10},{... | collective-permute-start | bytes 4718600 | tf_op jit(solution)/shard_map/ppermute | solution.py:14
  425.0 0.0 all-gather.10.cloned.1.call-done
  425.0 10.3 %fusion.28 = (f32[1024,768]{0,1:T(8,128)}, f32[1024,768]{0,1:T(8,128)}) fusion(bf16[3072,768]{1,0:T(8,128)(2,1)} %all-gather.10.cloned.1.call-done, bf16[1,1024,3072]{2,1,0:T(8,128)(2,1)} %all-gather.8.cloned.1.call-done), kind=kOutput, calls=%fused_computation.48 | convolution fusion | flops 4832624640 | bytes 17301504 | tf_op jit(solution)/shard_map/dot_general | solution.py:58
  435.3 3.5 copy.13
  438.8 2.3 reduce_sum.47
  441.1 56.1 %collective-permute-done.2 = bf16[1,1024,768]{1,2,0:T(8,128)(2,1)} collective-permute-done((bf16[1,1024,768]{1,2,0:T(8,128)(2,1)}, bf16[1,1024,768]{1,2,0:T(8,128)(2,1)}, u32[]{:S(2)}, u32[]{:S(2)}) %collective-permute-start.2) | collective-permute-done | bytes 1572896 | tf_op jit(solution)/shard_map/ppermute | solution.py:14
  497.2 1.5 constant_dynamic-update-slice_fusion.7
  498.7 1.5 constant_dynamic-update-slice_fusion.6
  500.3 0.1 constant_dynamic-update-slice_fusion.5
  500.4 0.1 constant_dynamic-update-slice_fusion.4
  500.5 1.5 constant_dynamic-update-slice_fusion.3
  502.1 1.5 constant_dynamic-update-slice_fusion.2
  503.6 0.1 constant_dynamic-update-slice_fusion.1
  503.7 0.1 constant_dynamic-update-slice_fusion
  503.9 0.0 copy-start.3
  503.9 0.0 copy-start.4
  503.9 3.1 constant_dynamic-slice_fusion
  507.0 0.0 copy-done.3
  507.0 0.0 copy-done.4
  507.0 38.7 %multiply_reduce_fusion = (f32[6,1024]{1,0:T(8,128)S(1)}, f32[6,1024,4096]{2,1,0:T(8,128)}) fusion(bf16[4096,6,128]{0,2,1:T(8,128)(2,1)} %bitcast.46, f32[1024,6,128]{2,0,1:T(8,128)S(1)} %copy-done.3, f32[128]{0:T(128)S(1)} %copy-done.4, f32[1024,6]{0,1:T(8,128)S(1)} %add_sqrt_fusion.1), kind=kOutput, calls=%fused_computation.1 | convolution fusion | flops 6495135744 | bytes 110150144 | tf_op jit(solution)/shard_map/cqhd,ckhd->chqk/dot_general | solution.py:76
  545.7 31.2 %fusion = f32[6,1024]{1,0:T(8,128)S(1)} fusion(f32[6,1024,4096]{2,1,0:T(8,128)} %get-tuple-element.10, f32[6,1024]{1,0:T(8,128)S(1)} %broadcast_maximum_fusion), kind=kLoop, calls=%fused_computation.2 | loop fusion | flops 75491328 | bytes 100712448 | tf_op jit(solution)/shard_map/reduce_sum | solution.py:81
  576.9 0.0 all-gather.18.cloned.1.call-done
  577.0 8.9 %copy.15 = bf16[4096,768]{0,1:T(8,128)(2,1)} copy(bf16[4096,768]{1,0:T(8,128)(2,1)} %all-gather.18.cloned.1.call-done) | data formatting | bytes 12582912 | tf_op jit(solution)/shard_map/all_gather | solution.py:71
  585.8 35.3 %divide_convert_fusion = bf16[6,1024,128]{1,2,0:T(8,128)(2,1)S(1)} fusion(bf16[4096,6,128]{0,2,1:T(8,128)(2,1)} %bitcast.48, f32[6,1024,4096]{2,1,0:T(8,128)} %get-tuple-element.10, f32[6,1024]{1,0:T(8,128)S(1)} %broadcast_maximum_fusion, f32[6,1024]{1,0:T(8,128)S(1)} %fusion), kind=kOutput, calls=%fused_computation.24 | convolution fusion | flops 6519521280 | bytes 108576768 | tf_op jit(solution)/shard_map/chqk,ckhd->chqd/dot_general | solution.py:82
  621.1 0.0 all-gather.16.cloned.1.call-done
  621.1 9.4 %convert_bitcast_fusion = bf16[1,1024,3072]{2,1,0:T(8,128)(2,1)} fusion(bf16[1024,768]{0,1:T(8,128)(2,1)S(1)} %bitcast.55, bf16[768,3072]{1,0:T(8,128)(2,1)} %all-gather.16.cloned.1.call-done), kind=kOutput, calls=%fused_computation.11 | convolution fusion | flops 4834983936 | bytes 12582912 | tf_op jit(solution)/shard_map/dot_general | solution.py:94
  630.5 0.0 copy-start.5
  630.5 0.0 reduce-scatter.2.cloned.1.call-update
  630.6 89.4 %reduce-scatter.2.cloned.1.call-done = bf16[1,256,3072]{2,1,0:T(8,128)(2,1)} async-done(((bf16[1,1024,3072]{2,1,0:T(8,128)(2,1)}), bf16[1,256,3072]{2,1,0:T(8,128)(2,1)}) %reduce-scatter.2.cloned.1.call-update) | async-done | bytes 1572880 | tf_op jit(solution)/shard_map/reduce_scatter | solution.py:97
  719.9 0.0 copy-done.5
  719.9 2.9 multiply_convert_fusion
  722.9 0.0 copy-done.1
  (7 shorter events, 0.1 us)
Async XLA Ops:
  6.5 150.3 %copy-start = (f32[128]{0:T(128)S(1)}, f32[128]{0:T(128)}, u32[]{:S(2)}) copy-start(f32[128]{0:T(128)} %param.19) | copy-start | bytes 1540
  6.5 5.2 copy-start.2
  6.5 94.5 %all-gather.14.cloned.1.call-start = ((), (), s32[]{:S(2)}) async-start(), calls=%async_computation.4 | async-start | bytes 5898240 | tf_op jit(solution)/shard_map/all_gather | solution.py:56
  7.3 140.1 %all-gather.8.cloned.1.call-start = ((), (), s32[]{:S(2)}) async-start(), calls=%async_computation.1 | async-start | bytes 7864320 | tf_op jit(solution)/shard_map/all_gather | solution.py:48
  14.4 224.0 %all-gather.12.cloned.1.call-start = ((), (), s32[]{:S(2)}) async-start(), calls=%async_computation.3 | async-start | bytes 5898240 | tf_op jit(solution)/shard_map/all_gather | solution.py:55
  15.1 409.8 %all-gather.10.cloned.1.call-start = ((), (), s32[]{:S(2)}) async-start(), calls=%async_computation.2 | async-start | bytes 5898240 | tf_op jit(solution)/shard_map/all_gather | solution.py:54
  15.7 561.2 %all-gather.18.cloned.1.call-start = ((), (), s32[]{:S(2)}) async-start(), calls=%async_computation.7 | async-start | bytes 7864320 | tf_op jit(solution)/shard_map/all_gather | solution.py:71
  156.8 464.3 %all-gather.16.cloned.1.call-start = ((), (), s32[]{:S(2)}) async-start(), calls=%async_computation.5 | async-start | bytes 5898240 | tf_op jit(solution)/shard_map/all_gather | solution.py:68
  250.9 72.5 %collective-permute-start = (bf16[1,1024,768]{1,2,0:T(8,128)(2,1)S(1)}, bf16[1,1024,768]{1,2,0:T(8,128)(2,1)S(1)}, u32[]{:S(2)}, u32[]{:S(2)}) collective-permute-start(bf16[1,1024,768]{1,2,0:T(8,128)(2,1)S(1)} %bitcast.47), channel_id=1, source_target_pairs={{0,4},{4,8},{8,12},{12,0},{1,5},{5,9},{9,13},{13,1},{2,6},{6,10},{... | collective-permute-start | bytes 4718600 | tf_op jit(solution)/shard_map/ppermute | solution.py:14
  323.4 88.5 %collective-permute-start.1 = (bf16[1,1024,768]{1,2,0:T(8,128)(2,1)S(1)}, bf16[1,1024,768]{1,2,0:T(8,128)(2,1)}, u32[]{:S(2)}, u32[]{:S(2)}) collective-permute-start(bf16[1,1024,768]{1,2,0:T(8,128)(2,1)S(1)} %collective-permute-done), channel_id=1, source_target_pairs={{0,4},{4,8},{8,12},{12,0},{1,5},{5,9},{9,13},{13,1},{2,6},{6,10},{... | collective-permute-start | bytes 4718600 | tf_op jit(solution)/shard_map/ppermute | solution.py:14
  352.2 367.7 %reduce-scatter.2.cloned.1.call-start = ((), (), s32[]{:S(2)}) async-start(), calls=%async_computation.6 | async-start | bytes 7864320 | tf_op jit(solution)/shard_map/reduce_scatter | solution.py:97
  411.9 85.3 %collective-permute-start.2 = (bf16[1,1024,768]{1,2,0:T(8,128)(2,1)}, bf16[1,1024,768]{1,2,0:T(8,128)(2,1)}, u32[]{:S(2)}, u32[]{:S(2)}) collective-permute-start(bf16[1,1024,768]{1,2,0:T(8,128)(2,1)} %collective-permute-done.1), channel_id=1, source_target_pairs={{0,4},{4,8},{8,12},{12,0},{1,5},{5,9},{9,13},{13,1},{2,6},{6,10},{... | collective-permute-start | bytes 4718600 | tf_op jit(solution)/shard_map/ppermute | solution.py:14
  503.9 3.1 copy-start.3
  503.9 3.1 copy-start.4
  630.5 89.4 %copy-start.5 = (f32[1,3072]{1,0:T(1,128)S(1)}, f32[1,3072]{1,0:T(1,128)}, u32[]{:S(2)}) copy-start(f32[1,3072]{1,0:T(1,128)} %param.13) | copy-start | bytes 36868
  630.5 92.3 %copy-start.1 = (f32[128]{0:T(128)S(1)}, f32[128]{0:T(128)}, u32[]{:S(2)}) copy-start(f32[128]{0:T(128)} %param.19) | copy-start | bytes 1540
Sparse Core Ops, SparseCore 0:
  8.9 92.1 all-gather.13
  102.6 44.7 all-gather.7
  149.0 89.3 all-gather.11
  239.8 123.5 all-gather.9
  364.8 165.2 all-gather.17
  531.6 87.5 all-gather.15
  630.7 89.2 reduce-scatter.1
